TPU v7x, 128 devices: a whole 4x4x4 slice. The times are simulated.
128 devices in a mesh: front: 4 (over y), row: 4 (over z_lo, core), col: 8 (over x, z_hi).
Axes of the slice: x: 4, y: 4, z: 4 (z_hi: 2, z_lo: 2; z = z_hi * 2 + z_lo), core: 2. Of those that a mesh axis runs over, the one named last changes fastest.
Arguments:
- pivot_block: bfloat16 [4, 1024, 1024], P('front'), may hold values from -6 to 6
- border: bfloat16 [4, 8192, 1024], P('front', 'row'), may hold values from -6 to 6
- contrib: bfloat16 [4, 8192, 8192], P('front', 'row', 'col'), may hold values from -6 to 6
- inverses: bfloat16 [4, 4, 256, 256], P('front'), may hold values from -0.0625 to 0.0625
- row_tiles: int32 [4, 64], replicated, may hold values from 0 to 79, as said below
- col_tiles: int32 [4, 64], replicated, may hold values from 0 to 79, as said below
- owner: int32 [80], replicated, may hold values from 0 to 79, as said below
- schur_init: bfloat16 [10240, 10240], P(('front', 'row'), 'col'), may hold values from -6 to 6
- block: bfloat16 [10240, 512], P('col'), may hold values from -0.0625 to 0.0625
Outputs:
- schur: float32 [10240, 10240], P(('front', 'row'), 'col')
- product: float32 [10240, 512], P(('front', 'row', 'col'))
Inputs may be any that keep to these rules, and one draw needn't show every extreme that they name: owner is a permutation of 0 .. 79. For each front the 64 entries are distinct. With s = owner[row_tiles[f, i]], each front has exactly 4 entries in each group s // 5; among the 16 entries of one aligned block of a front at most 2 fall in one group, and that many in some block of every draw. For each front the 64 entries are distinct. With s = owner[col_tiles[f, j]], each front has exactly 8 entries in each group s // 10; among the 8 entries of one aligned block of a front at most 2 fall in one group, and that many in some block of every draw.
All inputs are finite; a program needn't handle non-finite values.
Results may differ from a plain program's by a relative error of at most 0.008.
Values may be sent and summed in bfloat16 or wider, within the bound.
A program may use at most 128 MiB of HBM per device.

v0:
```python
import jax
import jax.numpy as jnp
from jax import lax
from jax.sharding import PartitionSpec as P

TILE = 128


def in_blocks(x, dim, length):
    before, after = (x.shape[:dim], x.shape[dim + 1 :])
    return jnp.moveaxis(x.reshape(*before, length, -1, *after), dim, 0)


def sent_and_summed(x, axis, dim):
    tiles = in_blocks(x, dim, lax.axis_size(axis))
    arrived = lax.all_to_all(tiles, axis, split_axis=0, concat_axis=0, tiled=True)
    return arrived.sum(axis=0)


def eliminate(pivot, rows, inverse_set):
    panels = inverse_set.shape[0]
    width = inverse_set.shape[1]
    pivot_now = pivot.astype(jnp.float32)
    rows_now = rows.astype(jnp.float32)
    leaves = []
    for panel_index in range(panels):
        start = panel_index * width
        left = pivot_now[:, start : start + width].astype(jnp.bfloat16)
        below = jnp.arange(pivot.shape[0])[:, None] >= start + width
        lower = jnp.where(
            below, jnp.dot(left, inverse_set[panel_index], preferred_element_type=jnp.float32), 0.0
        ).astype(jnp.bfloat16)
        side = jnp.dot(
            rows_now[:, start : start + width].astype(jnp.bfloat16),
            inverse_set[panel_index],
            preferred_element_type=jnp.float32,
        ).astype(jnp.bfloat16)
        pivot_now = pivot_now - lax.dot_general(
            lower, lower, (((1,), (1,)), ((), ())), preferred_element_type=jnp.float32
        )
        rows_now = rows_now - lax.dot_general(
            side, lower, (((1,), (1,)), ((), ())), preferred_element_type=jnp.float32
        )
        leaves.append(side)
    return jnp.concatenate(leaves, axis=1)


def route_tables(slots, per_group):
    group = slots // per_group
    within = slots % per_group
    count = slots.shape[-1]
    same = group[..., :, None] == group[..., None, :]
    earlier = jnp.arange(count)[None, :] < jnp.arange(count)[:, None]
    rank = jnp.sum((same & earlier).astype(jnp.int32), axis=-1)
    return (group, rank, within)


def pick_sources(group, rank, n_groups, capacity):
    count = group.shape[-1]
    match = (group[None, None, :] == jnp.arange(n_groups)[:, None, None]) & (
        rank[None, None, :] == jnp.arange(capacity)[None, :, None]
    )
    return jnp.sum(match.astype(jnp.int32) * jnp.arange(count)[None, None, :], axis=-1)


def shards(pivot_block, border, contrib, inverses, row_tiles, col_tiles, owner, schur_init, block):
    n_front = lax.axis_size("front")
    n_row = lax.axis_size("row")
    n_col = lax.axis_size("col")
    front_index = lax.axis_index("front")
    row_index = lax.axis_index("row")
    col_index = lax.axis_index("col")
    groups = n_front * n_row
    tiles_all = row_tiles.shape[1]
    slots_all = owner.shape[0]
    row_span = border.shape[1]
    col_span = contrib.shape[2]
    tile_rows = row_span // TILE
    tile_cols = col_span // TILE
    rows_per_group = slots_all // groups
    cols_per_group = slots_all // n_col
    cap_rows = 2 * tiles_all // (n_row * groups)
    cap_cols = 2 * tiles_all // (n_col * n_col)
    share = row_span // n_col
    own_rows = lax.dynamic_slice_in_dim(border[0], col_index * share, share, 0)
    leaves = eliminate(pivot_block[0], own_rows, inverses[0])
    factor = lax.all_gather(leaves, ("row", "col"), axis=0, tiled=True)
    mine = lax.dynamic_slice_in_dim(factor, row_index * row_span, row_span, 0)
    theirs = lax.dynamic_slice_in_dim(factor, col_index * col_span, col_span, 0)
    update = (
        contrib[0].astype(jnp.float32)
        - lax.dot_general(
            mine, theirs, (((1,), (1,)), ((), ())), preferred_element_type=jnp.float32
        )
    ).astype(jnp.bfloat16)
    tiles = update.reshape(tile_rows, TILE, tile_cols, TILE)
    slot_rows = owner[row_tiles].reshape(n_front, n_row, tile_rows)
    slot_cols = owner[col_tiles].reshape(n_front, n_col, tile_cols)
    group_rows, rank_rows, within_rows = route_tables(slot_rows, rows_per_group)
    group_cols, rank_cols, within_cols = route_tables(slot_cols, cols_per_group)
    send_rows = pick_sources(
        group_rows[front_index, row_index], rank_rows[front_index, row_index], groups, cap_rows
    )
    my_group = front_index * n_row + row_index
    flat_group = group_rows.reshape(groups, tile_rows)
    flat_rank = rank_rows.reshape(groups, tile_rows)
    flat_within = within_rows.reshape(groups, tile_rows)
    hit_rows = (flat_group == my_group)[:, None, :] & (
        flat_rank[:, None, :] == jnp.arange(cap_rows)[None, :, None]
    )
    place_rows = jnp.sum(
        (
            hit_rows[None]
            & (flat_within[None, :, None, :] == jnp.arange(rows_per_group)[:, None, None, None])
        ).astype(jnp.int32),
        axis=-1,
    ).astype(jnp.bfloat16)
    hit_cols = (group_cols == col_index)[:, :, None, :] & (
        rank_cols[:, :, None, :] == jnp.arange(cap_cols)[None, None, :, None]
    )
    place_cols = jnp.sum(
        (
            hit_cols[None]
            & (
                within_cols[None, :, :, None, :]
                == jnp.arange(cols_per_group)[:, None, None, None, None]
            )
        ).astype(jnp.int32),
        axis=-1,
    ).astype(jnp.bfloat16)
    place_cols = jnp.repeat(place_cols, n_row, axis=1)
    send_cols = pick_sources(
        group_cols[front_index, col_index], rank_cols[front_index, col_index], n_col, cap_cols
    )
    by_rows = jnp.take(tiles, send_rows.reshape(-1), axis=0)
    by_both = jnp.take(by_rows, send_cols.reshape(-1), axis=2)
    outgoing = by_both.reshape(groups, cap_rows, TILE, n_col, cap_cols, TILE).transpose(
        0, 3, 1, 4, 2, 5
    )
    outgoing = outgoing.reshape(groups * n_col, cap_rows, cap_cols, TILE, TILE)
    received = lax.all_to_all(
        outgoing, ("front", "row", "col"), split_axis=0, concat_axis=0, tiled=True
    )
    received = received.reshape(groups, n_col, cap_rows, cap_cols, TILE, TILE)
    gathered = jnp.einsum(
        "bgcm,gckmxy->bgkxy", place_cols, received, preferred_element_type=jnp.float32
    ).astype(jnp.bfloat16)
    summed = jnp.einsum("agk,bgkxy->abxy", place_rows, gathered, preferred_element_type=jnp.float32)
    schur = schur_init.astype(jnp.float32) + summed.transpose(0, 2, 1, 3).reshape(
        rows_per_group * TILE, cols_per_group * TILE
    )
    rounded = schur.astype(jnp.bfloat16)
    product = sent_and_summed(jnp.dot(rounded, block, preferred_element_type=jnp.float32), "col", 0)
    return (schur, product)


def solution(mesh):
    in_specs = (
        P("front", None, None),
        P("front", "row", None),
        P("front", "row", "col"),
        P("front", None, None, None),
        P(),
        P(),
        P(),
        P(("front", "row"), "col"),
        P("col", None),
    )
    out_specs = (P(("front", "row"), "col"), P(("front", "row", "col"), None))
    return jax.shard_map(shards, mesh=mesh, in_specs=in_specs, out_specs=out_specs, check_vma=False)
```

profile of v0, /device:TPU:0, one launch (start us, length us, event | category | flops | bytes accessed | tf_op | source)
XLA Modules:
  0.0 539.3 jit_solution(2947707500783428051)
XLA Ops:
  7.3 1.2 dynamic-slice_bitcast_fusion
  8.5 1.1 convolution_convert_fusion.3
  9.7 1.4 fusion.19
  12.8 2.7 fusion.59
  16.7 2.2 fusion.22
  18.9 1.1 convolution_convert_fusion
  20.1 1.8 pad_maximum_fusion
  22.0 2.0 gather_fusion
  25.3 1.9 gather_fusion.1
  28.7 117.7 %all-gather.2.cloned.1.call-done = bf16[8192,1024]{0,1:T(8,128)(2,1)} async-done(((bf16[256,1024]{0,1:T(8,128)(2,1)}), bf16[8192,1024]{0,1:T(8,128)(2,1)}) %all-gather.2.cloned.1.call-update) | async-done | bytes 16777232 | tf_op jit(solution)/shard_map/all_gather | solution.py:87
  146.4 8.7 %fusion.8 = bf16[256,8,8,128]{3,1,2,0:T(8,128)(2,1)S(1)} fusion(bf16[1,2048,1024]{2,1,0:T(8,128)(2,1)} %param.11, bf16[8192,1024]{0,1:T(8,128)(2,1)} %all-gather.2.cloned.1.call-done, s32[]{:T(128)S(6)} %select_n.153, s32[]{:T(128)S(6)} %select_n.154), kind=kOutput, calls=%fused_computation.14 | convolution fusion | flops 4301258752 | bytes 14680072 | tf_op jit(solution)/shard_map/dot_general | solution.py:92
  155.1 3.1 copy.39
  158.2 7.2 %gather_fusion.2 = bf16[32,128,8,128]{3,2,1,0:T(8,128)(2,1)} fusion(bf16[16,128,8,128]{3,2,1,0:T(8,128)(2,1)} %bitcast.87, s32[1024]{0:T(1024)S(1)} %pad_clamp_fusion.1), kind=kCustom, calls=%fused_computation.2 | custom fusion | bytes 16777344 | tf_op jit(solution)/shard_map/jit(_take)/gather | solution.py:135
  165.4 7.5 %broadcast_select_fusion = bf16[32,128,8,128]{3,2,1,0:T(8,128)(2,1)} fusion(bf16[32,128,8,128]{3,2,1,0:T(8,128)(2,1)} %gather_fusion.2, pred[32]{0:T(512)(128)(4,1)S(1)} %compare_and_fusion.2), kind=kLoop, calls=%fused_computation.13 | loop fusion | flops 4194304 | bytes 16777248 | tf_op jit(solution)/shard_map/jit(_take)/select_n | solution.py:135
  172.8 8.8 %copy.26 = bf16[32,128,8,128]{3,1,0,2:T(8,128)(2,1)} copy(bf16[32,128,8,128]{3,2,1,0:T(8,128)(2,1)} %broadcast_select_fusion) | data formatting | bytes 16777216 | tf_op jit(solution)/shard_map/jit(_take)/select_n | solution.py:135
  181.7 10.4 %gather_fusion.3 = bf16[16,32,128,128]{3,2,1,0:T(8,128)(2,1)} fusion(bf16[32,128,8,128]{3,1,0,2:T(8,128)(2,1)} %copy.26, s32[1024]{0:T(1024)S(1)} %pad_clamp_fusion), kind=kCustom, calls=%fused_computation.3 | custom fusion | bytes 33554496 | tf_op jit(solution)/shard_map/jit(_take)/gather | solution.py:136
  192.1 14.1 %copy_select_fusion = bf16[16,2,128,8,2,128]{5,2,4,1,3,0:T(8,128)(2,1)} fusion(bf16[16,2,128,8,2,128]{5,2,1,0,4,3:T(8,128)(2,1)} %bitcast.86, pred[8,2]{1,0:T(8,128)(4,1)S(1)} %copy.22), kind=kLoop, calls=%fused_computation.8 | loop fusion | flops 8388608 | bytes 33554448 | tf_op jit(solution)/shard_map/jit(_take)/select_n | solution.py:136
  206.2 11.1 %all-to-all-start = ((bf16[128,2,2,128,128]{4,3,2,1,0:T(8,128)(2,1)}), bf16[128,2,2,128,128]{4,3,2,1,0:T(8,128)(2,1)}, u32[]{:S(2)}, u32[]{:S(2)}) async-start(bf16[128,2,2,128,128]{4,3,2,1,0:T(8,128)(2,1)} %bitcast.85), calls=%async_computation | async-start | bytes 33554432 | tf_op jit(solution)/shard_map/all_to_all | solution.py:141
  218.2 235.2 %all-to-all-done = bf16[128,2,2,128,128]{4,3,2,1,0:T(8,128)(2,1)} async-done(((bf16[128,2,2,128,128]{4,3,2,1,0:T(8,128)(2,1)}), bf16[128,2,2,128,128]{4,3,2,1,0:T(8,128)(2,1)}, u32[]{:S(2)}, u32[]{:S(2)}) %all-to-all-start) | async-done | bytes 16777248 | tf_op jit(solution)/shard_map/all_to_all | solution.py:141
  453.4 25.6 %fusion = bf16[10,16,2,128,128]{4,0,3,2,1:T(8,128)(2,1)} fusion(bf16[10,16,8,2,1,1]{0,2,3,5,4,1:T(8,128)(2,1)S(1)} %bitcast.91, bf16[16,8,2,2,128,128]{5,4,3,2,1,0:T(8,128)(2,1)} %bitcast.19), kind=kOutput, calls=%fused_computation.5 | convolution fusion | flops 173015040 | bytes 27268096 | tf_op jit(solution)/shard_map/bgcm,gckmxy->bgkxy/dot_general | solution.py:145
  479.1 18.8 %fusion.11 = f32[5,128,10,128]{3,0,1,2:T(8,128)S(1)} fusion(bf16[10,16,2,128,128]{4,0,3,2,1:T(8,128)(2,1)} %fusion, bf16[5,16,2,1,1]{1,2,0,4,3:T(2,128)(2,1)S(1)} %convert_bitcast_fusion), kind=kOutput, calls=%fused_computation.19 | convolution fusion | flops 52428800 | bytes 13762880 | tf_op jit(solution)/shard_map/agk,bgkxy->abxy/dot_general | solution.py:148
  497.9 2.0 copy.32
  499.9 1.7 bitcast_add_fusion
  503.3 28.4 %all_to_all.10 = f32[8,80,512]{2,1,0:T(8,128)S(1)} all-to-all(f32[8,80,512]{2,1,0:T(8,128)S(1)} %bitcast.90), channel_id=1, replica_groups=mesh['front'=4,'row'=4,'col'=8] {'col'}, dimensions={0} | all-to-all | bytes 2621440 | tf_op jit(solution)/shard_map/all_to_all | solution.py:16
  (91 shorter events, 9.1 us)
Async XLA Ops:
  7.2 494.4 %copy-start = (bf16[1280,512]{1,0:T(8,128)(2,1)S(1)}, bf16[1280,512]{1,0:T(8,128)(2,1)}, u32[]{:S(2)}) copy-start(bf16[1280,512]{1,0:T(8,128)(2,1)} %param.17) | copy-start | bytes 3932164
  7.2 3.9 copy-start.4
  7.2 139.2 %all-gather.2.cloned.1.call-start = ((), (), s32[]{:S(2)}) async-start(), calls=%async_computation.2 | async-start | bytes 17301504 | tf_op jit(solution)/shard_map/all_gather | solution.py:87
  11.1 1.1 copy-start.6
  11.8 3.7 copy-start.2
  12.4 3.4 copy-start.7
  15.5 6.4 %copy-start.8 = (s32[4,64]{1,0:T(4,128)S(1)}, s32[4,64]{1,0:T(4,128)}, u32[]{:S(2)}) copy-start(s32[4,64]{1,0:T(4,128)} %param.14) | copy-start | bytes 3076
  15.5 6.4 %copy-start.9 = (s32[4,64]{1,0:T(4,128)S(1)}, s32[4,64]{1,0:T(4,128)}, u32[]{:S(2)}) copy-start(s32[4,64]{1,0:T(4,128)} %param.13) | copy-start | bytes 3076
  15.5 6.5 %copy-start.1 = (s32[80]{0:T(128)S(1)}, s32[80]{0:T(128)}, u32[]{:S(2)}) copy-start(s32[80]{0:T(128)} %param.15) | copy-start | bytes 964
  206.2 247.2 %all-to-all-start = ((bf16[128,2,2,128,128]{4,3,2,1,0:T(8,128)(2,1)}), bf16[128,2,2,128,128]{4,3,2,1,0:T(8,128)(2,1)}, u32[]{:S(2)}, u32[]{:S(2)}) async-start(bf16[128,2,2,128,128]{4,3,2,1,0:T(8,128)(2,1)} %bitcast.85), calls=%async_computation | async-start | bytes 33554432 | tf_op jit(solution)/shard_map/all_to_all | solution.py:141
  497.9 2.0 copy-start.5
  501.6 1.7 copy-start.3
Sparse Core Ops, SparseCore 0:
  22.0 124.3 all-gather.1
where the time goes:
time: 540 us; the launch traced here: 539 us
  waiting for transfers between devices  353 us (65%)
  matrix products  65.5 us (12%)
  local copies, waits for them, and re-layouts  38.8 us (7%)
  blocking collectives  28.4 us (5%)
  other arithmetic  28 us (5%)
  between operations  14.5 us (3%)
  starting transfers between devices  11.1 us (2%)
    all_to_all x1, waiting for transfers between devices, shards(): lax.all_to_all(outgoing, ('front', 'row', 'col'), split_axis=0, concat_ax...  235 us
    all_gather x1, waiting for transfers between devices, shards(): factor = lax.all_gather(leaves, ('row', 'col'), axis=0, tiled=True)  118 us
    all_to_all x1, blocking collectives, sent_and_summed(): lax.all_to_all(tiles, axis, split_axis=0, concat_axis=0, tiled=True)  28.4 us
    dot_general x1, matrix products, shards(): jnp.einsum('bgcm,gckmxy->bgkxy', place_cols, received, preferred_element_...  25.6 us
    dot_general x1, matrix products, shards(): jnp.einsum('agk,bgkxy->abxy', place_rows, gathered, preferred_element_typ...  18.8 us
    select_n x2, other arithmetic, shards(): by_both = jnp.take(by_rows, send_cols.reshape(-1), axis=2)  14.1 us
    all_to_all x1, starting transfers between devices, shards(): lax.all_to_all(outgoing, ('front', 'row', 'col'), split_axis=0, concat_ax...  11.1 us
  transfers between devices with their start and end apart: 2, of which 2 were waited for; matrix products, arithmetic and copies ran while one was open for 1% of the time, Pallas kernels for 0%

commit v1 on v0

--- a/solution.py
+++ b/solution.py
@@ -84,7 +84,10 @@
     share = row_span // n_col
     own_rows = lax.dynamic_slice_in_dim(border[0], col_index * share, share, 0)
     leaves = eliminate(pivot_block[0], own_rows, inverses[0])
-    factor = lax.all_gather(leaves, ("row", "col"), axis=0, tiled=True)
+    size = lax.axis_size(("row", "col"))
+    blocks = jnp.stack([leaves for _ in range(size)])
+    blocks = lax.all_to_all(blocks, ("row", "col"), split_axis=0, concat_axis=0)
+    factor = jnp.concatenate(blocks, axis=0)
     mine = lax.dynamic_slice_in_dim(factor, row_index * row_span, row_span, 0)
     theirs = lax.dynamic_slice_in_dim(factor, col_index * col_span, col_span, 0)
     update = (

time: 540 us -> 664 us (1.23)
  waiting for transfers between devices: 353 us -> 454 us
  starting transfers between devices: 11.1 us -> 35 us
  between operations: 14.5 us -> 1.4 us
    all_to_all x0 -> x1, waiting for transfers between devices: none -> 226 us  [shards(): blocks = lax.all_to_all(blocks, ('row', 'col'), split_axis=0, concat_axis=0)]
    all_gather x1 -> x0, waiting for transfers between devices: 118 us -> none  [shards(): factor = lax.all_gather(leaves, ('row', 'col'), axis=0, tiled=True)]
    all_to_all x1, starting transfers between devices: 11.1 us -> 26.2 us  [shards(): lax.all_to_all(outgoing, ('front', 'row', 'col'), split_axis=0, concat_ax...]
    all_to_all x0 -> x1, starting transfers between devices: none -> 8.83 us  [shards(): blocks = lax.all_to_all(blocks, ('row', 'col'), split_axis=0, concat_axis=0)]
    all_to_all x1, waiting for transfers between devices: 235 us -> 228 us  [shards(): lax.all_to_all(outgoing, ('front', 'row', 'col'), split_axis=0, concat_ax...]
where the time goes in v1:
time: 664 us; the launch traced here: 660 us
  waiting for transfers between devices  454 us (68%)
  matrix products  65.6 us (10%)
  local copies, waits for them, and re-layouts  44.8 us (7%)
  starting transfers between devices  35 us (5%)
  blocking collectives  32.1 us (5%)
  other arithmetic  27.2 us (4%)
    all_to_all x1, waiting for transfers between devices, shards(): lax.all_to_all(outgoing, ('front', 'row', 'col'), split_axis=0, concat_ax...  228 us
    all_to_all x1, waiting for transfers between devices, shards(): blocks = lax.all_to_all(blocks, ('row', 'col'), split_axis=0, concat_axis=0)  226 us
    all_to_all x1, blocking collectives, sent_and_summed(): lax.all_to_all(tiles, axis, split_axis=0, concat_axis=0, tiled=True)  32.1 us
    all_to_all x1, starting transfers between devices, shards(): lax.all_to_all(outgoing, ('front', 'row', 'col'), split_axis=0, concat_ax...  26.2 us
    dot_general x1, matrix products, shards(): jnp.einsum('bgcm,gckmxy->bgkxy', place_cols, received, preferred_element_...  25.6 us
    dot_general x1, matrix products, shards(): jnp.einsum('agk,bgkxy->abxy', place_rows, gathered, preferred_element_typ...  18.9 us
    select_n x2, other arithmetic, shards(): by_both = jnp.take(by_rows, send_cols.reshape(-1), axis=2)  14.1 us
  transfers between devices with their start and end apart: 2, of which 2 were waited for; matrix products, arithmetic and copies ran while one was open for 1% of the time, Pallas kernels for 0%

profile of v1, /device:TPU:0, one launch (start us, length us, event | category | flops | bytes accessed | tf_op | source)
XLA Modules:
  0.0 660.1 jit_solution(2626341979953435082)
XLA Ops:
  0.7 1.2 dynamic-slice_bitcast_fusion
  1.9 1.1 convolution_convert_fusion.3
  3.1 1.4 fusion.19
  6.2 2.7 fusion.59
  10.1 2.2 fusion.22
  14.7 6.0 stack.2
  20.7 8.8 %all-to-all-start = ((bf16[32,256,1024]{2,1,0:T(8,128)(2,1)}), bf16[32,256,1024]{2,1,0:T(8,128)(2,1)}, u32[]{:S(2)}, u32[]{:S(2)}) async-start(bf16[32,256,1024]{2,1,0:T(8,128)(2,1)} %stack.2), calls=%async_computation | async-start | bytes 33554432 | tf_op jit(solution)/shard_map/all_to_all | solution.py:89
  29.6 1.9 gather_fusion
  32.7 1.9 gather_fusion.1
  36.2 226.2 %all-to-all-done = bf16[32,256,1024]{2,1,0:T(8,128)(2,1)} async-done(((bf16[32,256,1024]{2,1,0:T(8,128)(2,1)}), bf16[32,256,1024]{2,1,0:T(8,128)(2,1)}, u32[]{:S(2)}, u32[]{:S(2)}) %all-to-all-start) | async-done | bytes 16777248 | tf_op jit(solution)/shard_map/all_to_all | solution.py:89
  262.4 8.7 %fusion.8 = bf16[256,8,8,128]{3,1,2,0:T(8,128)(2,1)S(1)} fusion(bf16[1,2048,1024]{2,1,0:T(8,128)(2,1)} %param.11, bf16[8192,1024]{1,0:T(8,128)(2,1)} %bitcast.13, s32[]{:T(128)S(6)} %select_n.153, s32[]{:T(128)S(6)} %select_n.154), kind=kOutput, calls=%fused_computation.14 | convolution fusion | flops 4301258752 | bytes 14680072 | tf_op jit(solution)/shard_map/dot_general | solution.py:95
  271.1 3.1 copy.44
  274.1 7.2 %gather_fusion.2 = bf16[32,128,8,128]{3,2,1,0:T(8,128)(2,1)} fusion(bf16[16,128,8,128]{3,2,1,0:T(8,128)(2,1)} %bitcast.88, s32[1024]{0:T(1024)S(1)} %pad_clamp_fusion.1), kind=kCustom, calls=%fused_computation.2 | custom fusion | bytes 16777344 | tf_op jit(solution)/shard_map/jit(_take)/gather | solution.py:138
  281.3 7.5 %broadcast_select_fusion = bf16[32,128,8,128]{3,2,1,0:T(8,128)(2,1)} fusion(bf16[32,128,8,128]{3,2,1,0:T(8,128)(2,1)} %gather_fusion.2, pred[32]{0:T(512)(128)(4,1)S(1)} %compare_and_fusion.2), kind=kLoop, calls=%fused_computation.13 | loop fusion | flops 4194304 | bytes 16777248 | tf_op jit(solution)/shard_map/jit(_take)/select_n | solution.py:138
  288.8 8.8 %copy.31 = bf16[32,128,8,128]{3,1,0,2:T(8,128)(2,1)} copy(bf16[32,128,8,128]{3,2,1,0:T(8,128)(2,1)} %broadcast_select_fusion) | data formatting | bytes 16777216 | tf_op jit(solution)/shard_map/jit(_take)/select_n | solution.py:138
  297.6 10.4 %gather_fusion.3 = bf16[16,32,128,128]{3,2,1,0:T(8,128)(2,1)} fusion(bf16[32,128,8,128]{3,1,0,2:T(8,128)(2,1)} %copy.31, s32[1024]{0:T(1024)S(1)} %pad_clamp_fusion), kind=kCustom, calls=%fused_computation.3 | custom fusion | bytes 33554496 | tf_op jit(solution)/shard_map/jit(_take)/gather | solution.py:139
  308.0 14.1 %copy_select_fusion = bf16[16,2,128,8,2,128]{5,2,4,1,3,0:T(8,128)(2,1)} fusion(bf16[16,2,128,8,2,128]{5,2,1,0,4,3:T(8,128)(2,1)} %bitcast.87, pred[8,2]{1,0:T(8,128)(4,1)S(1)} %copy.26), kind=kLoop, calls=%fused_computation.8 | loop fusion | flops 8388608 | bytes 33554448 | tf_op jit(solution)/shard_map/jit(_take)/select_n | solution.py:139
  322.1 26.2 %all-to-all-start.1 = ((bf16[128,2,2,128,128]{4,3,2,1,0:T(8,128)(2,1)}), bf16[128,2,2,128,128]{4,3,2,1,0:T(8,128)(2,1)}, u32[]{:S(2)}, u32[]{:S(2)}) async-start(bf16[128,2,2,128,128]{4,3,2,1,0:T(8,128)(2,1)} %bitcast.86), calls=%async_computation.1 | async-start | bytes 33554432 | tf_op jit(solution)/shard_map/all_to_all | solution.py:144
  349.2 227.7 %all-to-all-done.1 = bf16[128,2,2,128,128]{4,3,2,1,0:T(8,128)(2,1)} async-done(((bf16[128,2,2,128,128]{4,3,2,1,0:T(8,128)(2,1)}), bf16[128,2,2,128,128]{4,3,2,1,0:T(8,128)(2,1)}, u32[]{:S(2)}, u32[]{:S(2)}) %all-to-all-start.1) | async-done | bytes 16777248 | tf_op jit(solution)/shard_map/all_to_all | solution.py:144
  577.0 25.6 %fusion = bf16[10,16,2,128,128]{4,0,3,2,1:T(8,128)(2,1)} fusion(bf16[10,16,8,2,1,1]{0,2,3,5,4,1:T(8,128)(2,1)S(1)} %bitcast.92, bf16[16,8,2,2,128,128]{5,4,3,2,1,0:T(8,128)(2,1)} %bitcast.20), kind=kOutput, calls=%fused_computation.5 | convolution fusion | flops 173015040 | bytes 27268096 | tf_op jit(solution)/shard_map/bgcm,gckmxy->bgkxy/dot_general | solution.py:148
  602.6 18.9 %fusion.11 = f32[5,128,10,128]{3,0,1,2:T(8,128)S(1)} fusion(bf16[10,16,2,128,128]{4,0,3,2,1:T(8,128)(2,1)} %fusion, bf16[5,16,2,1,1]{1,2,0,4,3:T(2,128)(2,1)S(1)} %convert_bitcast_fusion), kind=kOutput, calls=%fused_computation.19 | convolution fusion | flops 52428800 | bytes 13762880 | tf_op jit(solution)/shard_map/agk,bgkxy->abxy/dot_general | solution.py:151
  621.6 2.0 copy.37
  623.6 1.7 bitcast_add_fusion
  627.0 32.1 %all_to_all.15 = f32[8,80,512]{2,1,0:T(8,128)S(1)} all-to-all(f32[8,80,512]{2,1,0:T(8,128)S(1)} %bitcast.91), channel_id=1, replica_groups=mesh['front'=4,'row'=4,'col'=8] {'col'}, dimensions={0} | all-to-all | bytes 2621440 | tf_op jit(solution)/shard_map/all_to_all | solution.py:16
  (92 shorter events, 11.4 us)
Async XLA Ops:
  0.6 624.6 %copy-start = (bf16[1280,512]{1,0:T(8,128)(2,1)S(1)}, bf16[1280,512]{1,0:T(8,128)(2,1)}, u32[]{:S(2)}) copy-start(bf16[1280,512]{1,0:T(8,128)(2,1)} %param.17) | copy-start | bytes 3932164
  0.6 3.8 copy-start.4
  4.5 1.1 copy-start.6
  5.2 3.6 copy-start.2
  5.9 3.4 copy-start.7
  20.6 8.8 %copy-start.8 = (s32[4,64]{1,0:T(4,128)S(1)}, s32[4,64]{1,0:T(4,128)}, u32[]{:S(2)}) copy-start(s32[4,64]{1,0:T(4,128)} %param.14) | copy-start | bytes 3076
  20.6 8.9 %copy-start.9 = (s32[4,64]{1,0:T(4,128)S(1)}, s32[4,64]{1,0:T(4,128)}, u32[]{:S(2)}) copy-start(s32[4,64]{1,0:T(4,128)} %param.13) | copy-start | bytes 3076
  20.7 9.0 %copy-start.1 = (s32[80]{0:T(128)S(1)}, s32[80]{0:T(128)}, u32[]{:S(2)}) copy-start(s32[80]{0:T(128)} %param.15) | copy-start | bytes 964
  20.7 241.7 %all-to-all-start = ((bf16[32,256,1024]{2,1,0:T(8,128)(2,1)}), bf16[32,256,1024]{2,1,0:T(8,128)(2,1)}, u32[]{:S(2)}, u32[]{:S(2)}) async-start(bf16[32,256,1024]{2,1,0:T(8,128)(2,1)} %stack.2), calls=%async_computation | async-start | bytes 33554432 | tf_op jit(solution)/shard_map/all_to_all | solution.py:89
  322.1 254.9 %all-to-all-start.1 = ((bf16[128,2,2,128,128]{4,3,2,1,0:T(8,128)(2,1)}), bf16[128,2,2,128,128]{4,3,2,1,0:T(8,128)(2,1)}, u32[]{:S(2)}, u32[]{:S(2)}) async-start(bf16[128,2,2,128,128]{4,3,2,1,0:T(8,128)(2,1)} %bitcast.86), calls=%async_computation.1 | async-start | bytes 33554432 | tf_op jit(solution)/shard_map/all_to_all | solution.py:144
  621.6 2.0 copy-start.5
  625.3 1.7 copy-start.3
